TPU v7x, 32 devices: a whole 2x2x4 slice. The times are simulated.
32 devices in a mesh: grp: 4 (over y, x), sub: 8 (over z, core).
Axes of the slice: x: 2, y: 2, z: 4, core: 2. Of those that a mesh axis runs over, the one named last changes fastest.
Arguments:
- bem_tiles: float32 [4096, 4096], P('grp', 'sub'), may hold values from -0.0625 to 0.0625
- leaf_inverse: float32 [4, 16, 1024, 1024], P('grp', 'sub'), may hold values from -1.5 to 1.5
- coupling: float32 [4, 16, 1024, 512], P('grp', 'sub'), may hold values from -0.0625 to 0.0625
- schur_inverse: float32 [4, 512, 512], P('grp', None, 'sub'), may hold values from -1.5 to 1.5
- leaf_load: float32 [4, 16, 1024, 128], P('grp', 'sub'), may hold values from -6 to 6
- sep_load: float32 [4, 512, 128], P('grp'), may hold values from -6 to 6
- surf_load: float32 [4096, 128], P(('grp', 'sub')), may hold values from -6 to 6
- surf_start: float32 [4096, 128], P(('grp', 'sub')), may hold values from -6 to 6
- flux_weight: float32 [4, 16, 8, 128], P('grp', 'sub'), may hold values from 0.25 to 1
- trace_weight: float32 [4, 16, 8, 128], P('grp', 'sub'), may hold values from 0.25 to 1
- leaf_sizes: int32 [4, 16], P('grp', 'sub'), may hold values from 512 to 1024
- block_counts: int32 [4, 16], P('grp', 'sub'), may hold values from 4 to 8
- block_owner: int32 [4, 16, 8, 1], P('grp', 'sub'), may hold values from 0 to 7; in each aligned block of 16 rows (0 to 15, 16 to 31, ..., all dimensions but the last counted through in order) at most 2 rows name the same one
Outputs:
- solution: float32 [4, 16, 1024, 128], P('grp', 'sub')
- sep_value: float32 [4, 512, 128], P('grp', 'sub')
- pressure: float32 [4096, 128], P(('grp', 'sub'))
Inputs may be any that keep to these rules, and one draw needn't show every extreme that they name: `block_owner`: of the 16 entries of one device, live or not, at most 2 name the same owner, and some device has 2 entries naming one owner.
All inputs are finite; a program needn't handle non-finite values.
Results may differ from a plain program's by a relative error of at most 0.00018.
Values sent between devices are 32-bit elements; how exact they have to be, the bound alone decides.
A program may use at most 128 MiB of HBM per device.

v0:
```python
import jax
import jax.numpy as jnp
from jax import lax
from jax.sharding import PartitionSpec as P

CAP = 2
SWEEPS = 3


def on_device(
    bem_tiles,
    leaf_inverse,
    coupling,
    schur_inverse,
    leaf_load,
    sep_load,
    surf_load,
    surf_start,
    flux_weight,
    trace_weight,
    leaf_sizes,
    block_counts,
    block_owner,
):
    highest = lax.Precision.HIGHEST
    parts = lax.axis_size("sub")
    here = lax.axis_index("sub")
    width = surf_load.shape[0]
    loads = surf_load.shape[1]
    leaves = leaf_inverse.shape[1]
    order = leaf_inverse.shape[2]
    blocks = order // width
    entries = leaves * blocks
    separator = schur_inverse.shape[1]
    sep_share = schur_inverse.shape[2]
    row_mask = (jnp.arange(order, dtype=jnp.int32)[None, :] < leaf_sizes[0][:, None]).astype(
        jnp.float32
    )[:, :, None]
    active = (
        (jnp.arange(blocks, dtype=jnp.int32)[None, :] < block_counts[0][:, None])
        .astype(jnp.float32)
        .reshape(entries)
    )
    owner = block_owner[0, :, :, 0].reshape(entries)
    picker = (owner[:, None] == jnp.arange(parts, dtype=jnp.int32)[None, :]).astype(jnp.float32)
    live_pick = picker * active[:, None]
    flux_scale = flux_weight[0].reshape(entries, width)[:, :, None]
    trace_scale = (trace_weight[0].reshape(entries, width) * active[:, None])[:, :, None]
    position = jnp.arange(entries, dtype=jnp.int32)
    earlier = (position[:, None] > position[None, :]) & (owner[:, None] == owner[None, :])
    slot_index = jnp.sum(earlier.astype(jnp.int32), axis=1)
    target = owner * CAP + slot_index
    placing = (jnp.arange(parts * CAP, dtype=jnp.int32)[:, None] == target[None, :]).astype(
        jnp.float32
    )
    schur_full = lax.all_gather(schur_inverse[0], "sub", axis=1, tiled=True)
    pressure = surf_start
    sep_value = jnp.zeros((separator, loads), jnp.float32)
    solution = jnp.zeros((leaves, order, loads), jnp.float32)
    for sweep in range(SWEEPS):
        column = lax.all_gather(pressure, "grp", axis=0, tiled=True)

        def tile_product(start, count, column=column):
            return jnp.dot(bem_tiles, column, precision=highest, preferred_element_type=jnp.float32)

        applied = lax.psum_scatter(
            tile_product(jnp.int32(0), lax.axis_size("sub") * width),
            "sub",
            scatter_dimension=0,
            tiled=True,
        )
        surface_patch = lax.all_gather(pressure, "sub", axis=0, tiled=True).reshape(
            parts, width, loads
        )
        flux = jnp.einsum("eo,oil->eil", live_pick, surface_patch, precision=highest) * flux_scale
        flux = flux.reshape(leaves, order, loads)
        pulled = jnp.einsum("jrs,sl->jrl", coupling[0], sep_value, precision=highest)
        rhs = (leaf_load[0] - pulled - flux) * row_mask
        solution = jnp.einsum("jrc,jcl->jrl", leaf_inverse[0], rhs, precision=highest) * row_mask
        partial_sum = jnp.einsum("jrs,jrl->sl", coupling[0], solution, precision=highest)
        summed = lax.psum(partial_sum, "sub")
        sep_value = jnp.dot(
            schur_full, sep_load[0] - summed, precision=highest, preferred_element_type=jnp.float32
        )
        weighted = solution.reshape(entries, width, loads) * trace_scale
        outgoing = jnp.dot(
            placing,
            weighted.reshape(entries, width * loads),
            precision=highest,
            preferred_element_type=jnp.float32,
        )
        incoming = lax.all_to_all(
            outgoing.reshape(parts, CAP, width, loads),
            "sub",
            split_axis=0,
            concat_axis=0,
            tiled=True,
        )
        trace = jnp.sum(incoming, axis=(0, 1))
        pressure = surf_load + applied + trace
    sep_rows_out = lax.dynamic_slice_in_dim(sep_value, here * sep_share, sep_share, 0)
    return (solution[None], sep_rows_out[None], pressure)


def solution(mesh):
    return jax.shard_map(
        on_device,
        mesh=mesh,
        in_specs=(
            P("grp", "sub"),
            P("grp", "sub", None, None),
            P("grp", "sub", None, None),
            P("grp", None, "sub"),
            P("grp", "sub", None, None),
            P("grp", None, None),
            P(("grp", "sub"), None),
            P(("grp", "sub"), None),
            P("grp", "sub", None, None),
            P("grp", "sub", None, None),
            P("grp", "sub"),
            P("grp", "sub"),
            P("grp", "sub", None, None),
        ),
        out_specs=(P("grp", "sub", None, None), P("grp", "sub", None), P(("grp", "sub"), None)),
        check_vma=False,
    )
```

profile of v0, /device:TPU:0, one launch (start us, length us, event | category | flops | bytes accessed | tf_op | source)
XLA Modules:
  0.0 464.7 jit_solution(11380869395240890339)
XLA Ops:
  7.3 10.9 %all_gather.23 = f32[512,128]{1,0:T(8,128)S(1)} all-gather(f32[128,128]{1,0:T(8,128)} %param.20), channel_id=1, replica_groups=mesh['grp'=4,'sub'=8] {'grp'}, dimensions={0}, use_global_device_ids=true | all-gather | bytes 327680 | tf_op jit(solution)/shard_map/all_gather | solution.py:61
  18.2 2.6 fusion.127
  20.8 15.6 %all_gather.21 = f32[1024,128]{1,0:T(8,128)S(1)} all-gather(f32[128,128]{1,0:T(8,128)} %param.20), channel_id=1, replica_groups=mesh['grp'=4,'sub'=8] {'sub'}, dimensions={0}, use_global_device_ids=true | all-gather | bytes 589824 | tf_op jit(solution)/shard_map/all_gather | solution.py:72
  39.7 1.3 copy.80
  41.0 1.6 copy.75
  42.6 7.2 %fusion.51 = f32[2,1024,128]{1,2,0:T(8,128)S(1)} fusion(f32[2,1024,128]{1,2,0:T(8,128)} %copy.80, f32[1,2,1024,512]{3,2,1,0:T(8,128)} %param.15, f32[1,2,1024,128]{2,3,1,0:T(8,128)S(1)} %copy.75, f32[2,1024]{1,0:T(2,128)S(1)} %compare_convert_fusion), kind=kOutput, calls=%fused_computation.29 | convolution fusion | flops 1611399168 | bytes 7348224 | tf_op jit(solution)/shard_map/jrs,sl->jrl/dot_general | solution.py:77
  49.8 12.1 %fusion.57 = f32[2,1024,128]{1,2,0:T(8,128)} fusion(f32[2,1024,128]{1,2,0:T(8,128)S(1)} %fusion.51, f32[1,2,1024,1024]{3,2,1,0:T(8,128)} %param.14, f32[2,1024]{1,0:T(2,128)S(1)} %compare_convert_fusion), kind=kOutput, calls=%fused_computation.34 | convolution fusion | flops 3221487616 | bytes 10493952 | tf_op jit(solution)/shard_map/jrc,jcl->jrl/dot_general | solution.py:79
  62.0 1.6 copy.81
  65.0 2.4 fusion.85
  68.7 5.2 %all-to-all-start = ((f32[8,2,128,128]{3,2,1,0:T(8,128)}), f32[8,2,128,128]{3,2,1,0:T(8,128)}, u32[]{:S(2)}, u32[]{:S(2)}) async-start(f32[8,2,128,128]{3,2,1,0:T(8,128)} %copy.83), calls=%async_computation.1 | async-start | bytes 2097152 | tf_op jit(solution)/shard_map/all_to_all | solution.py:92
  74.3 5.7 %fusion.69 = f32[512,128]{0,1:T(8,128)} fusion(f32[2,1024,128]{1,2,0:T(8,128)} %fusion.57, f32[1,2,1024,512]{3,2,1,0:T(8,128)} %param.15), kind=kOutput, calls=%fused_computation.40 | convolution fusion | flops 1610612736 | bytes 5505024 | tf_op jit(solution)/shard_map/jrs,jrl->sl/dot_general | solution.py:80
  81.8 20.1 %all-to-all-done = f32[8,2,128,128]{3,2,1,0:T(8,128)} async-done(((f32[8,2,128,128]{3,2,1,0:T(8,128)}), f32[8,2,128,128]{3,2,1,0:T(8,128)}, u32[]{:S(2)}, u32[]{:S(2)}) %all-to-all-start) | async-done | bytes 1048608 | tf_op jit(solution)/shard_map/all_to_all | solution.py:92
  101.9 1.9 reduce_sum.37
  104.8 14.8 %all_gather.24 = f32[1024,128]{1,0:T(8,128)S(1)} all-gather(f32[128,128]{1,0:T(8,128)S(1)} %add_add_fusion.2), channel_id=1, replica_groups=mesh['grp'=4,'sub'=8] {'sub'}, dimensions={0}, use_global_device_ids=true | all-gather | bytes 589824 | tf_op jit(solution)/shard_map/all_gather | solution.py:72
  119.5 1.8 convolution_multiply_fusion.1
  122.7 2.6 copy.86
  125.2 15.9 %all-reduce.4.cloned.1.call-done = f32[512,128]{0,1:T(8,128)} async-done(((f32[512,128]{0,1:T(8,128)}), f32[512,128]{0,1:T(8,128)}) %all-reduce.4.cloned.1.call-update) | async-done | bytes 262160 | tf_op jit(solution)/shard_map/psum | solution.py:81
  141.2 22.9 %all-gather.3.cloned.1.call-done = f32[1,512,512]{1,2,0:T(8,128)} async-done(((f32[1,512,64]{1,2,0:T(8,128)}), f32[1,512,512]{1,2,0:T(8,128)}) %all-gather.3.cloned.1.call-update) | async-done | bytes 1048592 | tf_op jit(solution)/shard_map/all_gather | solution.py:56
  164.1 2.0 convolution_bitcast_fusion.3
  166.1 7.2 %fusion.42 = f32[2,1024,128]{1,2,0:T(8,128)S(1)} fusion(f32[2,1024,128]{1,2,0:T(8,128)} %copy.86, f32[128,512,1]{1,0,2:T(8,128)S(1)} %convolution_bitcast_fusion.3, f32[1,2,1024,512]{3,2,1,0:T(8,128)} %param.15, f32[1,2,1024,128]{2,3,1,0:T(8,128)} %copy-done.2, f32[2,1024]{1,0:T(2,128)S(1)} %compare_convert_fusion), kind=kOutput, calls=%fused_computation.26 | convolution fusion | flops 1611399168 | bytes 7610368 | tf_op jit(solution)/shard_map/jrs,sl->jrl/dot_general | solution.py:77
  173.3 12.1 %fusion.63 = f32[2,1024,128]{1,2,0:T(8,128)} fusion(f32[2,1024,128]{1,2,0:T(8,128)S(1)} %fusion.42, f32[1,2,1024,1024]{3,2,1,0:T(8,128)} %param.14, f32[2,1024]{1,0:T(2,128)S(1)} %compare_convert_fusion), kind=kOutput, calls=%fused_computation.36 | convolution fusion | flops 3221487616 | bytes 10493952 | tf_op jit(solution)/shard_map/jrc,jcl->jrl/dot_general | solution.py:79
  185.4 2.6 copy.88
  188.0 2.4 reshape.166
  190.4 2.5 fusion.83
  194.0 4.2 all-to-all-start.1
  198.5 5.7 %fusion.72 = f32[512,128]{0,1:T(8,128)} fusion(f32[2,1024,128]{1,2,0:T(8,128)} %fusion.63, f32[1,2,1024,512]{3,2,1,0:T(8,128)} %param.15), kind=kOutput, calls=%fused_computation.41 | convolution fusion | flops 1610612736 | bytes 5505024 | tf_op jit(solution)/shard_map/jrs,jrl->sl/dot_general | solution.py:80
  204.2 9.0 %all_gather.25 = f32[512,128]{1,0:T(8,128)S(1)} all-gather(f32[128,128]{1,0:T(8,128)S(1)} %add_add_fusion.2), channel_id=1, replica_groups=mesh['grp'=4,'sub'=8] {'grp'}, dimensions={0}, use_global_device_ids=true | all-gather | bytes 327680 | tf_op jit(solution)/shard_map/all_gather | solution.py:61
  213.2 3.1 convolution_bitcast_fusion.1
  216.3 1.6 copy.87
  217.9 48.1 %all-reduce.6.cloned.1.call-done = f32[512,128]{0,1:T(8,128)} async-done(((f32[512,128]{0,1:T(8,128)}), f32[512,128]{0,1:T(8,128)}) %all-reduce.6.cloned.1.call-update) | async-done | bytes 262160 | tf_op jit(solution)/shard_map/psum | solution.py:81
  266.0 2.7 convolution_bitcast_fusion.2
  270.8 28.2 %reduce-scatter.6.cloned.1.call-done = f32[128,128]{0,1:T(8,128)} async-done(((f32[1024,128]{0,1:T(8,128)}), f32[128,128]{0,1:T(8,128)}) %reduce-scatter.6.cloned.1.call-update) | async-done | bytes 65552 | tf_op jit(solution)/shard_map/reduce_scatter | solution.py:66
  299.9 14.9 %all_gather.26 = f32[1024,128]{0,1:T(8,128)S(1)} all-gather(f32[128,128]{0,1:T(8,128)S(1)} %add_add_fusion.1), channel_id=1, replica_groups=mesh['grp'=4,'sub'=8] {'sub'}, dimensions={0}, use_global_device_ids=true | all-gather | bytes 589824 | tf_op jit(solution)/shard_map/all_gather | solution.py:72
  315.7 2.0 copy.93
  317.8 2.1 convolution_multiply_fusion
  321.1 2.6 copy.95
  323.7 7.2 %fusion.33 = f32[2,1024,128]{1,2,0:T(8,128)S(1)} fusion(f32[2,1024,128]{1,2,0:T(8,128)} %copy.95, f32[128,512,1]{1,0,2:T(8,128)} %convolution_bitcast_fusion.2, f32[1,2,1024,512]{3,2,1,0:T(8,128)} %param.15, f32[1,2,1024,128]{2,3,1,0:T(8,128)} %copy-done.2, f32[2,1024]{1,0:T(2,128)S(1)} %compare_convert_fusion), kind=kOutput, calls=%fused_computation.23 | convolution fusion | flops 1611399168 | bytes 7610368 | tf_op jit(solution)/shard_map/jrs,sl->jrl/dot_general | solution.py:77
  330.9 12.1 %fusion.66 = f32[2,128,1024]{2,1,0:T(8,128)} fusion(f32[2,1024,128]{1,2,0:T(8,128)S(1)} %fusion.33, f32[1,2,1024,1024]{3,2,1,0:T(8,128)} %param.14, f32[2,1024]{1,0:T(2,128)S(1)} %compare_convert_fusion), kind=kOutput, calls=%fused_computation.37 | convolution fusion | flops 3221487616 | bytes 10493952 | tf_op jit(solution)/shard_map/jrc,jcl->jrl/dot_general | solution.py:79
  343.0 2.6 copy.97
  345.7 2.4 reshape.169
  348.1 2.4 fusion.81
  351.7 4.2 all-to-all-start.2
  356.2 5.3 %fusion.75 = f32[512,128]{0,1:T(8,128)} fusion(f32[1,2,1024,512]{3,2,1,0:T(8,128)} %param.15, f32[2,128,1024]{2,1,0:T(8,128)S(1)} %copy-done.1), kind=kOutput, calls=%fused_computation.42 | convolution fusion | flops 1610612736 | bytes 5505024 | tf_op jit(solution)/shard_map/jrs,jrl->sl/dot_general | solution.py:80
  361.6 10.3 %all_gather.27 = f32[512,128]{0,1:T(8,128)S(1)} all-gather(f32[128,128]{0,1:T(8,128)S(1)} %add_add_fusion.1), channel_id=1, replica_groups=mesh['grp'=4,'sub'=8] {'grp'}, dimensions={0}, use_global_device_ids=true | all-gather | bytes 327680 | tf_op jit(solution)/shard_map/all_gather | solution.py:61
  371.9 3.1 convolution_bitcast_fusion
  376.3 47.2 %all-reduce.8.cloned.1.call-done = f32[512,128]{0,1:T(8,128)} async-done(((f32[512,128]{0,1:T(8,128)}), f32[512,128]{0,1:T(8,128)}) %all-reduce.8.cloned.1.call-update) | async-done | bytes 262160 | tf_op jit(solution)/shard_map/psum | solution.py:81
  423.6 3.1 fusion.87
  428.7 27.4 %reduce-scatter.8.cloned.1.call-done = f32[128,128]{0,1:T(8,128)} async-done(((f32[1024,128]{0,1:T(8,128)}), f32[128,128]{0,1:T(8,128)}) %reduce-scatter.8.cloned.1.call-update) | async-done | bytes 65552 | tf_op jit(solution)/shard_map/reduce_scatter | solution.py:66
  (73 shorter events, 23.6 us)
Async XLA Ops:
  7.2 11.0 %copy-start = (f32[1024,512]{1,0:T(8,128)S(1)}, f32[1024,512]{1,0:T(8,128)}, u32[]{:S(2)}) copy-start(f32[1024,512]{1,0:T(8,128)} %param.13) | copy-start | bytes 6291460
  7.2 29.7 %copy-start.9 = (s32[1,2,8,1]{2,3,1,0:T(1,128)S(1)}, s32[1,2,8,1]{2,3,1,0:T(1,128)}, u32[]{:S(2)}) copy-start(s32[1,2,8,1]{2,3,1,0:T(1,128)} %param.25) | copy-start | bytes 196
  7.2 30.6 %copy-start.11 = (s32[1,2]{1,0:T(1,128)S(1)}, s32[1,2]{1,0:T(1,128)}, u32[]{:S(2)}) copy-start(s32[1,2]{1,0:T(1,128)} %param.24) | copy-start | bytes 28
  7.2 30.8 %copy-start.10 = (s32[1,2]{1,0:T(1,128)S(1)}, s32[1,2]{1,0:T(1,128)}, u32[]{:S(2)}) copy-start(s32[1,2]{1,0:T(1,128)} %param.23) | copy-start | bytes 28
  7.2 30.8 %copy-start.4 = (f32[1,2,8,128]{3,2,1,0:T(8,128)S(1)}, f32[1,2,8,128]{3,2,1,0:T(8,128)}, u32[]{:S(2)}) copy-start(f32[1,2,8,128]{3,2,1,0:T(8,128)} %param.21) | copy-start | bytes 24580
  7.2 30.9 %copy-start.5 = (f32[1,2,8,128]{3,2,1,0:T(8,128)S(1)}, f32[1,2,8,128]{3,2,1,0:T(8,128)}, u32[]{:S(2)}) copy-start(f32[1,2,8,128]{3,2,1,0:T(8,128)} %param.22) | copy-start | bytes 24580
  7.2 96.6 %reduce-scatter.4.cloned.1.call-start = ((), (), s32[]{:S(2)}) async-start(), calls=%async_computation.7 | async-start | bytes 589824 | tf_op jit(solution)/shard_map/reduce_scatter | solution.py:66
  37.6 24.3 %copy-start.6 = (s32[16]{0:T(128)}, s32[16]{0:T(128)S(1)}, u32[]{:S(2)}) copy-start(s32[16]{0:T(128)S(1)} %eq.58) | copy-start | bytes 196
  42.6 19.3 %copy-start.2 = (f32[1,2,1024,128]{2,3,1,0:T(8,128)}, f32[1,2,1024,128]{2,3,1,0:T(8,128)S(1)}, u32[]{:S(2)}) copy-start(f32[1,2,1024,128]{2,3,1,0:T(8,128)S(1)} %copy.75) | copy-start | bytes 3145732
  61.9 5.5 %copy-start.7 = (s32[16]{0:T(128)}, s32[16]{0:T(128)S(1)}, u32[]{:S(2)}) copy-start(s32[16]{0:T(128)S(1)} %multiply_add_fusion.1) | copy-start | bytes 196
  68.7 33.3 %all-to-all-start = ((f32[8,2,128,128]{3,2,1,0:T(8,128)}), f32[8,2,128,128]{3,2,1,0:T(8,128)}, u32[]{:S(2)}, u32[]{:S(2)}) async-start(f32[8,2,128,128]{3,2,1,0:T(8,128)} %copy.83), calls=%async_computation.1 | async-start | bytes 2097152 | tf_op jit(solution)/shard_map/all_to_all | solution.py:92
  73.8 67.3 %all-reduce.4.cloned.1.call-start = ((), (), s32[]{:S(2)}) async-start(), calls=%async_computation.6 | async-start | bytes 524288 | tf_op jit(solution)/shard_map/psum | solution.py:81
  80.0 84.1 %all-gather.3.cloned.1.call-start = ((), (), s32[]{:S(2)}) async-start(), calls=%async_computation.12 | async-start | bytes 1179648 | tf_op jit(solution)/shard_map/all_gather | solution.py:56
  194.0 74.8 %all-to-all-start.1 = ((f32[8,2,128,128]{3,2,1,0:T(8,128)}), f32[8,2,128,128]{3,2,1,0:T(8,128)}, u32[]{:S(2)}, u32[]{:S(2)}) async-start(f32[8,2,128,128]{3,2,1,0:T(8,128)} %copy.90), calls=%async_computation.3 | async-start | bytes 2097152 | tf_op jit(solution)/shard_map/all_to_all | solution.py:92
  198.3 67.8 %all-reduce.6.cloned.1.call-start = ((), (), s32[]{:S(2)}) async-start(), calls=%async_computation.8 | async-start | bytes 524288 | tf_op jit(solution)/shard_map/psum | solution.py:81
  204.2 94.8 %reduce-scatter.6.cloned.1.call-start = ((), (), s32[]{:S(2)}) async-start(), calls=%async_computation.9 | async-start | bytes 589824 | tf_op jit(solution)/shard_map/reduce_scatter | solution.py:66
  343.0 5.0 %copy-start.8 = (s32[16]{0:T(128)S(1)}, s32[16]{0:T(128)}, u32[]{:S(2)}) copy-start(s32[16]{0:T(128)} %copy-done.7) | copy-start | bytes 196
  350.5 5.7 %copy-start.1 = (f32[2,128,1024]{2,1,0:T(8,128)S(1)}, f32[2,128,1024]{2,1,0:T(8,128)}, u32[]{:S(2)}) copy-start(f32[2,128,1024]{2,1,0:T(8,128)} %fusion.66) | copy-start | bytes 3145732
  351.7 75.6 %all-to-all-start.2 = ((f32[8,2,128,128]{3,2,1,0:T(8,128)}), f32[8,2,128,128]{3,2,1,0:T(8,128)}, u32[]{:S(2)}, u32[]{:S(2)}) async-start(f32[8,2,128,128]{3,2,1,0:T(8,128)} %copy.99), calls=%async_computation.5 | async-start | bytes 2097152 | tf_op jit(solution)/shard_map/all_to_all | solution.py:92
  356.0 67.6 %all-reduce.8.cloned.1.call-start = ((), (), s32[]{:S(2)}) async-start(), calls=%async_computation.10 | async-start | bytes 524288 | tf_op jit(solution)/shard_map/psum | solution.py:81
  361.6 94.5 %reduce-scatter.8.cloned.1.call-start = ((), (), s32[]{:S(2)}) async-start(), calls=%async_computation.11 | async-start | bytes 589824 | tf_op jit(solution)/shard_map/reduce_scatter | solution.py:66
  371.9 84.2 %copy-start.3 = (f32[128,128]{0,1:T(8,128)S(1)}, f32[128,128]{0,1:T(8,128)}, u32[]{:S(2)}) copy-start(f32[128,128]{0,1:T(8,128)} %copy.87) | copy-start | bytes 196612
Sparse Core Ops, SparseCore 0:
  20.9 31.6 reduce-scatter.3
  80.1 61.0 all-reduce.3
  142.8 21.2 all-gather.2
  204.3 61.7 all-reduce.5
  268.7 30.1 reduce-scatter.5
  361.7 61.8 all-reduce.7
  425.8 30.1 reduce-scatter.7
where the time goes:
time: 468 us; the launch traced here: 465 us
  waiting for transfers between devices  211 us (45%)
  matrix products  104 us (22%)
  blocking collectives  75.4 us (16%)
  local copies, waits for them, and re-layouts  37.4 us (8%)
  starting transfers between devices  14.7 us (3%)
  between operations  14.6 us (3%)
  other arithmetic  8.24 us (2%)
    psum x3, waiting for transfers between devices, on_device(): summed = lax.psum(partial_sum, 'sub')  111 us
    reduce_scatter x3, waiting for transfers between devices, on_device(): lax.psum_scatter(tile_product(jnp.int32(0), lax.axis_size('sub') * width)...  55.5 us
    all_gather x3, blocking collectives, on_device(): lax.all_gather(pressure, 'sub', axis=0, tiled=True)  45.3 us
    dot_general x3, matrix products, on_device(): jnp.einsum('jrc,jcl->jrl', leaf_inverse[0], rhs, precision=highest)  36.3 us
    all_gather x3, blocking collectives, on_device(): column = lax.all_gather(pressure, 'grp', axis=0, tiled=True)  30.1 us
    all_gather x1, waiting for transfers between devices, on_device(): schur_full = lax.all_gather(schur_inverse[0], 'sub', axis=1, tiled=True)  22.9 us
    dot_general x3, matrix products, on_device(): jnp.einsum('jrs,sl->jrl', coupling[0], sep_value, precision=highest)  21.6 us
    all_to_all x3, waiting for transfers between devices, on_device(): lax.all_to_all(outgoing.reshape(parts, CAP, width, loads), 'sub', split_a...  20.1 us
  transfers between devices with their start and end apart: 10, of which 7 were waited for; matrix products, arithmetic and copies ran while one was open for 17% of the time, Pallas kernels for 0%

commit v1 on v0

--- a/solution.py
+++ b/solution.py
@@ -22,7 +22,7 @@
     block_counts,
     block_owner,
 ):
-    highest = lax.Precision.HIGHEST
+    highest = lax.Precision.HIGH
     parts = lax.axis_size("sub")
     here = lax.axis_index("sub")
     width = surf_load.shape[0]
@@ -46,29 +46,13 @@
     live_pick = picker * active[:, None]
     flux_scale = flux_weight[0].reshape(entries, width)[:, :, None]
     trace_scale = (trace_weight[0].reshape(entries, width) * active[:, None])[:, :, None]
-    position = jnp.arange(entries, dtype=jnp.int32)
-    earlier = (position[:, None] > position[None, :]) & (owner[:, None] == owner[None, :])
-    slot_index = jnp.sum(earlier.astype(jnp.int32), axis=1)
-    target = owner * CAP + slot_index
-    placing = (jnp.arange(parts * CAP, dtype=jnp.int32)[:, None] == target[None, :]).astype(
-        jnp.float32
-    )
     schur_full = lax.all_gather(schur_inverse[0], "sub", axis=1, tiled=True)
     pressure = surf_start
     sep_value = jnp.zeros((separator, loads), jnp.float32)
     solution = jnp.zeros((leaves, order, loads), jnp.float32)
     for sweep in range(SWEEPS):
         column = lax.all_gather(pressure, "grp", axis=0, tiled=True)
-
-        def tile_product(start, count, column=column):
-            return jnp.dot(bem_tiles, column, precision=highest, preferred_element_type=jnp.float32)
-
-        applied = lax.psum_scatter(
-            tile_product(jnp.int32(0), lax.axis_size("sub") * width),
-            "sub",
-            scatter_dimension=0,
-            tiled=True,
-        )
+        product = jnp.dot(bem_tiles, column, precision=highest, preferred_element_type=jnp.float32)
         surface_patch = lax.all_gather(pressure, "sub", axis=0, tiled=True).reshape(
             parts, width, loads
         )
@@ -84,20 +68,14 @@
         )
         weighted = solution.reshape(entries, width, loads) * trace_scale
         outgoing = jnp.dot(
-            placing,
+            picker.T,
             weighted.reshape(entries, width * loads),
             precision=highest,
             preferred_element_type=jnp.float32,
         )
-        incoming = lax.all_to_all(
-            outgoing.reshape(parts, CAP, width, loads),
-            "sub",
-            split_axis=0,
-            concat_axis=0,
-            tiled=True,
+        pressure = surf_load + lax.psum_scatter(
+            product + outgoing.reshape(parts * width, loads), "sub", scatter_dimension=0, tiled=True
         )
-        trace = jnp.sum(incoming, axis=(0, 1))
-        pressure = surf_load + applied + trace
     sep_rows_out = lax.dynamic_slice_in_dim(sep_value, here * sep_share, sep_share, 0)
     return (solution[None], sep_rows_out[None], pressure)
 

time: 468 us -> 444 us (0.949); the launches traced: 465 us -> 436 us
  matrix products: 104 us -> 77.5 us
    all_to_all x3 -> x0, waiting for transfers between devices: 20.1 us -> none  [on_device(): lax.all_to_all(outgoing.reshape(parts, CAP, width, loads), 'sub', split_a...]
    reduce_scatter x3, waiting for transfers between devices: 55.5 us -> 72.4 us  [on_device(): lax.psum_scatter(product + outgoing.reshape(parts * width, loads), 'sub',...]
    dot_general x3, matrix products: 36.3 us -> 20.7 us  [on_device(): jnp.einsum('jrc,jcl->jrl', leaf_inverse[0], rhs, precision=highest)]
    all_to_all x3 -> x0, starting transfers between devices: 13.6 us -> none  [on_device(): lax.all_to_all(outgoing.reshape(parts, CAP, width, loads), 'sub', split_a...]
    psum x3, starting transfers between devices: 0.91 us -> 11.8 us  [on_device(): summed = lax.psum(partial_sum, 'sub')]
    dot_general x3, matrix products: 21.6 us -> 13.1 us  [on_device(): jnp.einsum('jrs,sl->jrl', coupling[0], sep_value, precision=highest)]
    reshape x3 -> x5, local copies, waits for them, and re-layouts: 6.44 us -> 9.99 us  [on_device(): outgoing.reshape(parts * width, loads)]
  transfers between devices with their start and end apart: 10 -> 7, of which waited for: 7 -> 7; matrix products, arithmetic and copies ran while one was open for 17% -> 8% of each run, Pallas kernels for 0% -> 0%
where the time goes in v1:
time: 444 us; the launch traced here: 436 us
  waiting for transfers between devices  212 us (48%)
  blocking collectives  77.6 us (17%)
  matrix products  77.5 us (17%)
  local copies, waits for them, and re-layouts  35.9 us (8%)
  between operations  14.8 us (3%)
  starting transfers between devices  12.2 us (3%)
  other arithmetic  6.1 us (1%)
    psum x3, waiting for transfers between devices, on_device(): summed = lax.psum(partial_sum, 'sub')  116 us
    reduce_scatter x3, waiting for transfers between devices, on_device(): lax.psum_scatter(product + outgoing.reshape(parts * width, loads), 'sub',...  72.4 us
    all_gather x3, blocking collectives, on_device(): lax.all_gather(pressure, 'sub', axis=0, tiled=True)  46.2 us
    all_gather x3, blocking collectives, on_device(): column = lax.all_gather(pressure, 'grp', axis=0, tiled=True)  31.3 us
    all_gather x1, waiting for transfers between devices, on_device(): schur_full = lax.all_gather(schur_inverse[0], 'sub', axis=1, tiled=True)  22.9 us
    dot_general x3, matrix products, on_device(): jnp.einsum('jrc,jcl->jrl', leaf_inverse[0], rhs, precision=highest)  20.7 us
    dot_general x3, matrix products, on_device(): jnp.einsum('jrs,jrl->sl', coupling[0], solution, precision=highest)  15 us
    dot_general x3, matrix products, on_device(): jnp.einsum('jrs,sl->jrl', coupling[0], sep_value, precision=highest)  13.1 us
  transfers between devices with their start and end apart: 7, of which 7 were waited for; matrix products, arithmetic and copies ran while one was open for 8% of the time, Pallas kernels for 0%

profile of v1, /device:TPU:0, one launch (start us, length us, event | category | flops | bytes accessed | tf_op | source)
XLA Modules:
  0.0 436.0 jit_solution(10881729736087087071)
XLA Ops:
  7.2 11.0 %all_gather.23 = f32[512,128]{1,0:T(8,128)S(1)} all-gather(f32[128,128]{1,0:T(8,128)} %param.20), channel_id=1, replica_groups=mesh['grp'=4,'sub'=8] {'grp'}, dimensions={0}, use_global_device_ids=true | all-gather | bytes 327680 | tf_op jit(solution)/shard_map/all_gather | solution.py:54
  18.3 16.3 %all_gather.21 = f32[1024,128]{1,0:T(8,128)} all-gather(f32[128,128]{1,0:T(8,128)} %param.20), channel_id=1, replica_groups=mesh['grp'=4,'sub'=8] {'sub'}, dimensions={0}, use_global_device_ids=true | all-gather | bytes 589824 | tf_op jit(solution)/shard_map/all_gather | solution.py:56
  35.0 1.3 reduce.3
  39.5 1.8 convolution_multiply_fusion.2
  41.7 4.2 fusion.51
  46.0 4.6 %fusion.57 = f32[2,1024,128]{1,2,0:T(8,128)S(1)} fusion(f32[2,1024,128]{2,1,0:T(8,128)S(1)} %fusion.51, f32[1,2,1024,1024]{3,2,1,0:T(8,128)S(1)} %copy-done.3, f32[2,1024]{1,0:T(2,128)S(1)} %compare_convert_fusion), kind=kOutput, calls=%fused_computation.34 | convolution fusion | flops 1610874880 | bytes 10493952 | tf_op jit(solution)/shard_map/jrc,jcl->jrl/dot_general | solution.py:63
  50.6 1.3 copy.30
  51.9 2.4 reshape.117
  54.6 2.9 fusion.80
  57.5 1.9 reshape.118
  59.5 2.9 convolution_add_fusion
  62.4 11.5 %all-reduce.4.cloned.1.call-start = ((), (), s32[]{:S(2)}) async-start(), calls=%async_computation.3 | async-start | bytes 524288 | tf_op jit(solution)/shard_map/psum | solution.py:65
  73.9 6.7 %fusion.71 = f32[512,128]{1,0:T(8,128)} fusion(f32[2,1024,128]{1,2,0:T(8,128)} %copy-done.6, f32[1,2,1024,512]{3,2,1,0:T(8,128)} %param.15), kind=kOutput, calls=%fused_computation.43 | convolution fusion | flops 805306368 | bytes 5505024 | tf_op jit(solution)/shard_map/jrs,jrl->sl/dot_general | solution.py:64
  81.4 12.4 %reduce-scatter.4.cloned.1.call-done = f32[128,128]{1,0:T(8,128)} async-done(((f32[1024,128]{1,0:T(8,128)}), f32[128,128]{1,0:T(8,128)}) %reduce-scatter.4.cloned.1.call-update) | async-done | bytes 65552 | tf_op jit(solution)/shard_map/reduce_scatter | solution.py:76
  94.7 15.2 %all_gather.24 = f32[1024,128]{1,0:T(8,128)S(1)} all-gather(f32[128,128]{1,0:T(8,128)S(1)} %add.34), channel_id=1, replica_groups=mesh['grp'=4,'sub'=8] {'sub'}, dimensions={0}, use_global_device_ids=true | all-gather | bytes 589824 | tf_op jit(solution)/shard_map/all_gather | solution.py:56
  111.9 9.6 %all_gather.25 = f32[512,128]{1,0:T(8,128)} all-gather(f32[128,128]{1,0:T(8,128)S(1)} %add.34), channel_id=1, replica_groups=mesh['grp'=4,'sub'=8] {'grp'}, dimensions={0}, use_global_device_ids=true | all-gather | bytes 327680 | tf_op jit(solution)/shard_map/all_gather | solution.py:54
  121.5 28.4 %all-reduce.4.cloned.1.call-done = f32[512,128]{1,0:T(8,128)} async-done(((f32[512,128]{1,0:T(8,128)}), f32[512,128]{1,0:T(8,128)}) %all-reduce.4.cloned.1.call-update) | async-done | bytes 262160 | tf_op jit(solution)/shard_map/psum | solution.py:65
  149.9 22.9 %all-gather.3.cloned.1.call-done = f32[1,512,512]{1,2,0:T(8,128)} async-done(((f32[1,512,64]{1,2,0:T(8,128)}), f32[1,512,512]{1,2,0:T(8,128)}) %all-gather.3.cloned.1.call-update) | async-done | bytes 1048592 | tf_op jit(solution)/shard_map/all_gather | solution.py:49
  172.8 1.8 convolution_bitcast_fusion.3
  174.6 4.6 %fusion.42 = f32[2,1024,128]{2,1,0:T(8,128)S(1)} fusion(f32[2,1024,128]{2,1,0:T(8,128)} %bitcast.188, f32[128,512,1]{1,0,2:T(8,128)S(1)} %convolution_bitcast_fusion.3, f32[1,2,1024,512]{3,2,1,0:T(8,128)} %param.15, f32[1,2,1024,128]{3,2,1,0:T(8,128)} %param.17, f32[2,1024]{1,0:T(2,128)S(1)} %compare_convert_fusion), kind=kOutput, calls=%fused_computation.26 | convolution fusion | flops 806092800 | bytes 7610368 | tf_op jit(solution)/shard_map/jrs,sl->jrl/dot_general | solution.py:61
  179.2 8.1 %fusion.63 = f32[2,1024,128]{1,2,0:T(8,128)S(1)} fusion(f32[2,1024,128]{2,1,0:T(8,128)S(1)} %fusion.42, f32[1,2,1024,1024]{3,2,1,0:T(8,128)} %param.14, f32[2,1024]{1,0:T(2,128)S(1)} %compare_convert_fusion), kind=kOutput, calls=%fused_computation.36 | convolution fusion | flops 1610874880 | bytes 10493952 | tf_op jit(solution)/shard_map/jrc,jcl->jrl/dot_general | solution.py:63
  188.3 4.2 fusion.74
  192.4 2.6 copy.34
  195.0 2.4 reshape.121
  197.4 2.9 fusion.81
  200.3 1.9 reshape.122
  202.2 2.1 copy.35
  204.3 3.1 fusion.69
  208.7 50.8 %all-reduce.6.cloned.1.call-done = f32[512,128]{1,0:T(8,128)} async-done(((f32[512,128]{1,0:T(8,128)}), f32[512,128]{1,0:T(8,128)}) %all-reduce.6.cloned.1.call-update) | async-done | bytes 262160 | tf_op jit(solution)/shard_map/psum | solution.py:65
  259.5 2.5 convolution_bitcast_fusion.2
  262.0 30.4 %reduce-scatter.6.cloned.1.call-done = f32[128,128]{0,1:T(8,128)} async-done(((f32[1024,128]{0,1:T(8,128)}), f32[128,128]{0,1:T(8,128)}) %reduce-scatter.6.cloned.1.call-update) | async-done | bytes 65552 | tf_op jit(solution)/shard_map/reduce_scatter | solution.py:76
  293.3 10.7 %all_gather.27 = f32[512,128]{0,1:T(8,128)} all-gather(f32[128,128]{0,1:T(8,128)S(1)} %add.36), channel_id=1, replica_groups=mesh['grp'=4,'sub'=8] {'grp'}, dimensions={0}, use_global_device_ids=true | all-gather | bytes 327680 | tf_op jit(solution)/shard_map/all_gather | solution.py:54
  303.9 14.8 %all_gather.26 = f32[1024,128]{0,1:T(8,128)S(1)} all-gather(f32[128,128]{0,1:T(8,128)S(1)} %add.36), channel_id=1, replica_groups=mesh['grp'=4,'sub'=8] {'sub'}, dimensions={0}, use_global_device_ids=true | all-gather | bytes 589824 | tf_op jit(solution)/shard_map/all_gather | solution.py:56
  319.7 2.1 copy.37
  321.7 1.7 convolution_multiply_fusion
  323.8 4.2 fusion.33
  328.0 8.1 %fusion.66 = f32[2,128,1024]{2,1,0:T(8,128)S(1)} fusion(f32[2,1024,128]{2,1,0:T(8,128)S(1)} %fusion.33, f32[1,2,1024,1024]{3,2,1,0:T(8,128)} %param.14, f32[2,1024]{1,0:T(2,128)S(1)} %compare_convert_fusion), kind=kOutput, calls=%fused_computation.37 | convolution fusion | flops 1610874880 | bytes 10493952 | tf_op jit(solution)/shard_map/jrc,jcl->jrl/dot_general | solution.py:63
  337.1 4.2 fusion.77
  341.6 2.5 copy.40
  344.1 2.4 reshape.125
  346.6 2.9 fusion.82
  349.5 2.0 reshape.126
  351.5 2.1 copy.41
  353.5 3.1 fusion.70
  356.7 1.3 copy.43
  358.0 36.7 %all-reduce.8.cloned.1.call-done = f32[512,128]{1,0:T(8,128)} async-done(((f32[512,128]{1,0:T(8,128)}), f32[512,128]{1,0:T(8,128)}) %all-reduce.8.cloned.1.call-update) | async-done | bytes 262160 | tf_op jit(solution)/shard_map/psum | solution.py:65
  394.7 2.3 fusion.83
  397.6 29.6 %reduce-scatter.8.cloned.1.call-done = f32[128,128]{0,1:T(8,128)} async-done(((f32[1024,128]{0,1:T(8,128)}), f32[128,128]{0,1:T(8,128)}) %reduce-scatter.8.cloned.1.call-update) | async-done | bytes 65552 | tf_op jit(solution)/shard_map/reduce_scatter | solution.py:76
  (56 shorter events, 15.9 us)
Async XLA Ops:
  7.2 52.3 %copy-start = (f32[1024,512]{1,0:T(8,128)S(1)}, f32[1024,512]{1,0:T(8,128)}, u32[]{:S(2)}) copy-start(f32[1024,512]{1,0:T(8,128)} %param.13) | copy-start | bytes 6291460
  7.2 34.5 %copy-start.8 = (f32[1,2,1024,128]{3,2,1,0:T(8,128)S(1)}, f32[1,2,1024,128]{3,2,1,0:T(8,128)}, u32[]{:S(2)}) copy-start(f32[1,2,1024,128]{3,2,1,0:T(8,128)} %param.17) | copy-start | bytes 3145732
  7.2 86.6 %reduce-scatter.4.cloned.1.call-start = ((), (), s32[]{:S(2)}) async-start(), calls=%async_computation.4 | async-start | bytes 589824 | tf_op jit(solution)/shard_map/reduce_scatter | solution.py:76
  41.3 4.6 %copy-start.3 = (f32[1,2,1024,1024]{3,2,1,0:T(8,128)S(1)}, f32[1,2,1024,1024]{3,2,1,0:T(8,128)}, u32[]{:S(2)}) copy-start(f32[1,2,1024,1024]{3,2,1,0:T(8,128)} %param.14) | copy-start | bytes 25165828
  50.6 1.3 copy-start.6
  59.5 34.3 %copy-start.11 = (f32[128,128]{1,0:T(8,128)S(1)}, f32[128,128]{1,0:T(8,128)}, u32[]{:S(2)}) copy-start(f32[128,128]{1,0:T(8,128)} %param.19) | copy-start | bytes 196612
  62.4 110.4 %copy-start.10 = (f32[1,512,128]{2,1,0:T(8,128)S(1)}, f32[1,512,128]{2,1,0:T(8,128)}, u32[]{:S(2)}) copy-start(f32[1,512,128]{2,1,0:T(8,128)} %param.18) | copy-start | bytes 786436
  62.4 87.5 %all-reduce.4.cloned.1.call-start = ((), (), s32[]{:S(2)}) async-start(), calls=%async_computation.3 | async-start | bytes 524288 | tf_op jit(solution)/shard_map/psum | solution.py:65
  80.6 92.2 %all-gather.3.cloned.1.call-start = ((), (), s32[]{:S(2)}) async-start(), calls=%async_computation.9 | async-start | bytes 1179648 | tf_op jit(solution)/shard_map/all_gather | solution.py:49
  81.3 178.1 %all-reduce.6.cloned.1.call-start = ((), (), s32[]{:S(2)}) async-start(), calls=%async_computation.5 | async-start | bytes 524288 | tf_op jit(solution)/shard_map/psum | solution.py:65
  179.2 9.1 %copy-start.1 = (f32[1,2,1024,512]{3,2,1,0:T(8,128)S(1)}, f32[1,2,1024,512]{3,2,1,0:T(8,128)}, u32[]{:S(2)}) copy-start(f32[1,2,1024,512]{3,2,1,0:T(8,128)} %param.15) | copy-start | bytes 12582916
  187.3 1.0 copy-start.7
  204.3 88.1 %reduce-scatter.6.cloned.1.call-start = ((), (), s32[]{:S(2)}) async-start(), calls=%async_computation.6 | async-start | bytes 589824 | tf_op jit(solution)/shard_map/reduce_scatter | solution.py:76
  207.5 187.2 %all-reduce.8.cloned.1.call-start = ((), (), s32[]{:S(2)}) async-start(), calls=%async_computation.7 | async-start | bytes 524288 | tf_op jit(solution)/shard_map/psum | solution.py:65
  321.7 2.1 copy-start.9
  328.0 9.1 %copy-start.2 = (f32[1,2,1024,512]{3,2,1,0:T(8,128)S(1)}, f32[1,2,1024,512]{3,2,1,0:T(8,128)}, u32[]{:S(2)}) copy-start(f32[1,2,1024,512]{3,2,1,0:T(8,128)} %param.15) | copy-start | bytes 12582916
  336.1 1.0 copy-start.4
  341.3 85.9 %reduce-scatter.8.cloned.1.call-start = ((), (), s32[]{:S(2)}) async-start(), calls=%async_computation.8 | async-start | bytes 589824 | tf_op jit(solution)/shard_map/reduce_scatter | solution.py:76
  349.5 7.2 %copy-start.5 = (f32[2,128,1024]{2,1,0:T(8,128)S(1)}, f32[2,128,1024]{2,1,0:T(8,128)}, u32[]{:S(2)}) copy-start(f32[2,128,1024]{2,1,0:T(8,128)} %copy-done.4) | copy-start | bytes 3145732
Sparse Core Ops, SparseCore 0:
  62.5 31.2 reduce-scatter.3
  96.1 53.6 all-reduce.3
  151.5 21.2 all-gather.2
  204.4 55.0 all-reduce.5
  262.2 30.1 reduce-scatter.5
  341.4 53.1 all-reduce.7
  396.9 30.1 reduce-scatter.7
